TPU v7x, 32 devices: a whole 2x2x4 slice. The times are simulated.
32 devices in a mesh: batch: 4 (over z), row: 4 (over x, core), col: 2 (over y).
Axes of the slice: x: 2, y: 2, z: 4, core: 2. Of those that a mesh axis runs over, the one named last changes fastest.
Arguments:
- embeddings: bfloat16 [512, 128, 512], P('batch', 'col', 'row'), may hold values from -170 to 170
- projection: bfloat16 [512, 32], replicated, may hold values from -0.25 to 0.25
- w_in: bfloat16 [16384, 2048], P('row', 'col'), may hold values from -0.046875 to 0.046875
- bias: float32 [2048], P('col'), may hold values from -3 to 3
- w_out: bfloat16 [2048, 128, 512], P(None, 'col', 'row'), may hold values from -0.125 to 0.125
- cotangent: bfloat16 [512, 128, 512], P('batch', 'col', 'row'), may hold values from -0.1796875 to 0.1796875
Outputs:
- mixed: bfloat16 [512, 128, 512], P('batch', 'col', 'row')
- grad_out: float32 [2048, 128, 512], P('batch', 'col', 'row')
- grad_in: float32 [16384, 2048], P('row', 'col')
- grad_bias: float32 [2048], P('col')
- grad_proj: float32 [512, 32], P('row')
All inputs are finite; a program needn't handle non-finite values.
Results may differ from a plain program's by a relative error of at most 0.006.
Values may be sent and summed in bfloat16 or wider, within the bound.
No kernel may reach another device: no remote copies, remote signals or barrier semaphores. Data moves between devices by JAX's collectives and lax.ppermute only.
A program may use at most 192 MiB of HBM per device.

v0:
```python
import jax
import jax.numpy as jnp
from jax import lax
from jax.sharding import PartitionSpec as P

epsilon = 1e-06


def contract_first(left, right):
    return lax.dot_general(
        left, right, (((0,), (0,)), ((), ())), preferred_element_type=jnp.float32
    )


def contract_last(left, right):
    return lax.dot_general(
        left, right, (((1,), (1,)), ((), ())), preferred_element_type=jnp.float32
    )


def local(embeddings, projection, w_in, bias, w_out, cotangent):
    highest = lax.Precision.HIGHEST
    tok_rows, feat_local, emb_local = embeddings.shape
    rank_cols = projection.shape[1]
    row_count = lax.axis_size("row")
    col_count = lax.axis_size("col")
    col_place = lax.axis_index("col")
    emb_float = embeddings.astype(jnp.float32)
    full_rows = lax.all_gather(embeddings, "col", axis=1, tiled=True)
    regrouped = lax.all_to_all(embeddings, "col", split_axis=2, concat_axis=1, tiled=True)
    column_rows = lax.all_gather(regrouped, "row", axis=2, tiled=True)
    tile_gram = jnp.einsum(
        "bdj,bde->bje", column_rows, full_rows, preferred_element_type=jnp.float32
    )
    block_size = emb_local // col_count
    stacked = projection.reshape(row_count, emb_local, rank_cols)
    chosen = lax.dynamic_slice_in_dim(stacked, col_place * block_size, block_size, 1)
    chosen = chosen.reshape(row_count * block_size, rank_cols).astype(jnp.float32)
    partial_value = jnp.einsum("bje,jk->bek", tile_gram, chosen, precision=highest)
    interact = lax.psum(partial_value, "col")
    feature_count = emb_local * row_count * rank_cols
    square_sum = lax.psum(jnp.sum(interact * interact, axis=(1, 2)), "row")
    inv_rms = lax.rsqrt(square_sum / feature_count + epsilon)[:, None, None]
    normed = interact * inv_rms
    activated = normed.astype(jnp.bfloat16).reshape(tok_rows, emb_local * rank_cols)
    preact = lax.psum(jnp.dot(activated, w_in, preferred_element_type=jnp.float32), "row") + bias
    hidden = jax.nn.silu(preact).astype(jnp.bfloat16)
    hidden_all = lax.all_gather(hidden, "col", axis=1, tiled=True)
    flat_out = w_out.reshape(w_out.shape[0], feat_local * emb_local)
    mixed = (
        jnp.dot(hidden_all, flat_out, preferred_element_type=jnp.float32)
        .astype(jnp.bfloat16)
        .reshape(tok_rows, feat_local, emb_local)
    )
    cot_rows = cotangent.reshape(tok_rows, feat_local * emb_local)
    d_cols = lax.psum_scatter(
        contract_last(cot_rows, flat_out), "col", scatter_dimension=1, tiled=True
    )
    d_hidden = lax.psum(d_cols, "row")
    sigmoid_pre = jax.nn.sigmoid(preact)
    d_preact = d_hidden * sigmoid_pre * (1.0 + preact * (1.0 - sigmoid_pre))
    d_pre_b = d_preact.astype(jnp.bfloat16)
    per_batch = w_out.shape[0] // lax.axis_size("batch")
    every_hidden, every_cot = (
        lax.all_gather(hidden_all, "batch", axis=0, tiled=True),
        lax.all_gather(cot_rows, "batch", axis=0, tiled=True),
    )
    own_hidden = lax.dynamic_slice_in_dim(
        every_hidden, lax.axis_index("batch") * per_batch, per_batch, 1
    )
    grad_flat = contract_first(own_hidden, every_cot)
    grad_out = grad_flat.reshape(per_batch, feat_local, emb_local)
    grad_in, grad_bias = lax.psum(
        (contract_first(activated, d_pre_b), jnp.sum(d_preact, axis=0)), "batch"
    )
    d_act = lax.psum(contract_last(d_pre_b, w_in), "col").reshape(tok_rows, emb_local, rank_cols)
    inner_term = lax.psum(jnp.sum(d_act * normed, axis=(1, 2)), "row") / feature_count
    d_inter = (inv_rms * (d_act - normed * inner_term[:, None, None])).astype(jnp.bfloat16)
    back_fold = lax.psum(
        jnp.einsum("bek,bde->bdk", d_inter, embeddings, preferred_element_type=jnp.float32), "row"
    )
    grad_proj = lax.psum(
        jnp.einsum("bde,bdk->ek", emb_float, back_fold, precision=highest), ("batch", "col")
    )
    return (mixed, grad_out, grad_in, grad_bias, grad_proj)


def solution(mesh):
    placed = (
        P("batch", "col", "row"),
        P(),
        P("row", "col"),
        P("col"),
        P(None, "col", "row"),
        P("batch", "col", "row"),
    )
    return jax.shard_map(
        local,
        mesh=mesh,
        in_specs=placed,
        out_specs=(
            P("batch", "col", "row"),
            P("batch", "col", "row"),
            P("row", "col"),
            P("col"),
            P("row", None),
        ),
        check_vma=False,
    )
```

profile of v0, /device:TPU:0, one launch (start us, length us, event | category | flops | bytes accessed | tf_op | source)
XLA Modules:
  0.0 1151.0 jit_solution(1242558977459168627)
XLA Ops:
  12.9 49.2 %all_to_all.18 = bf16[128,64,128]{0,1,2:T(8,128)(2,1)S(1)} all-to-all(bf16[128,64,128]{0,1,2:T(8,128)(2,1)} %copy.22), channel_id=1, replica_groups=mesh['batch'=4,'row'=4,'col'=2] {'col'}, dimensions={2} | all-to-all | bytes 4194304 | tf_op jit(solution)/shard_map/all_to_all | solution.py:30
  67.7 20.5 %all-gather.7.cloned.1.call-done = bf16[128,128,128]{2,1,0:T(8,128)(2,1)} async-done(((bf16[128,64,128]{2,1,0:T(8,128)(2,1)}), bf16[128,128,128]{2,1,0:T(8,128)(2,1)}) %all-gather.7.cloned.1.call-update) | async-done | bytes 4194320 | tf_op jit(solution)/shard_map/all_gather | solution.py:29
  88.2 60.9 %all-gather.5.cloned.1.call-done = bf16[128,128,256]{1,2,0:T(8,128)(2,1)} async-done(((bf16[128,128,64]{1,2,0:T(8,128)(2,1)}), bf16[128,128,256]{1,2,0:T(8,128)(2,1)}) %all-gather.5.cloned.1.call-update) | async-done | bytes 8388624 | tf_op jit(solution)/shard_map/all_gather | solution.py:31
  149.1 13.1 %fusion.24 = f32[128,256,128]{2,1,0:T(8,128)} fusion(bf16[128,128,256]{1,2,0:T(8,128)(2,1)} %all-gather.5.cloned.1.call-done, bf16[128,128,128]{2,1,0:T(8,128)(2,1)} %all-gather.7.cloned.1.call-done), kind=kOutput, calls=%fused_computation.32 | convolution fusion | flops 1073741824 | bytes 29360128 | tf_op jit(solution)/shard_map/bdj,bde->bje/dot_general | solution.py:32
  162.2 11.5 %fusion.25 = f32[128,128,32]{1,2,0:T(8,128)} fusion(f32[128,256,128]{2,1,0:T(8,128)} %fusion.24, bf16[256,32,1]{0,1,2:T(8,128)(2,1)S(1)} %reshape.45), kind=kOutput, calls=%fused_computation.33 | convolution fusion | flops 1610612736 | bytes 18890752 | tf_op jit(solution)/shard_map/bje,jk->bek/dot_general | solution.py:39
  175.3 21.4 %fusion.8 = f32[128,2048]{1,0:T(8,128)} fusion(bf16[2048,64,128]{2,1,0:T(8,128)(2,1)} %param.10, bf16[128,64,128]{2,1,0:T(8,128)(2,1)S(1)} %copy-done.3), kind=kOutput, calls=%fused_computation.7 | convolution fusion | flops 4294967296 | bytes 36700160 | tf_op jit(solution)/shard_map/dot_general | solution.py:16
  196.8 40.1 %all-reduce.7.cloned.1.call-done = f32[128,128,32]{1,2,0:T(8,128)} async-done(((f32[128,128,32]{1,2,0:T(8,128)}), f32[128,128,32]{1,2,0:T(8,128)}) %all-reduce.7.cloned.1.call-update) | async-done | bytes 2097168 | tf_op jit(solution)/shard_map/psum | solution.py:40
  239.7 6.8 psum.71
  250.2 5.5 fusion.26
  260.0 39.2 %all-reduce.15.cloned.1.call-done = (f32[128,1024]{1,0:T(8,128)}, f32[128,1024]{1,0:T(8,128)}) async-done(((f32[128,1024]{1,0:T(8,128)}, f32[128,1024]{1,0:T(8,128)}), (f32[128,1024]{1,0:T(8,128)}, f32[128,1024]{1,0:T(8,128)})) %all-reduce.15.cloned.1.call-update) | async-done | bytes 1048592 | tf_op jit(solution)/shard_map/psum | solution.py:46
  301.4 7.0 fusion.18
  311.8 63.5 %all-reduce.11.cloned.1.call-done = f32[128,128,32]{1,2,0:T(8,128)} async-done(((f32[128,128,32]{1,2,0:T(8,128)}), f32[128,128,32]{1,2,0:T(8,128)}) %all-reduce.11.cloned.1.call-update) | async-done | bytes 2097168 | tf_op jit(solution)/shard_map/psum | solution.py:76
  378.8 6.4 psum.77
  395.8 8.1 all_gather.17
  404.1 8.5 fusion.20
  413.6 26.8 %fusion.12 = bf16[16,8,64,128]{3,1,2,0:T(8,128)(2,1)} fusion(bf16[128,2048]{1,0:T(8,128)(2,1)S(1)} %copy-done.5, bf16[256,8,64,128]{3,2,1,0:T(8,128)(2,1)} %bitcast.60), kind=kOutput, calls=%fused_computation.14 | convolution fusion | flops 4296015872 | bytes 36175872 | tf_op jit(solution)/shard_map/dot_general | solution.py:51
  444.1 13.1 %psum.75 = f32[1024]{0:T(1024)} all-reduce(f32[1024]{0:T(1024)S(1)} %get-tuple-element.7), channel_id=1, replica_groups=mesh['batch'=4,'row'=4,'col'=2] {'batch'}, use_global_device_ids=true, to_apply=%region_8.9 | all-reduce | flops 1024 | bytes 8192 | tf_op jit(solution)/shard_map/psum | solution.py:73
  459.9 40.4 %psum.79 = f32[128,32]{0,1:T(8,128)} all-reduce(f32[128,32]{0,1:T(8,128)S(1)} %convolution_bitcast_fusion.2), channel_id=1, replica_groups=mesh['batch'=4,'row'=4,'col'=2] {'batch','col'}, use_global_device_ids=true, to_apply=%region_13.14 | all-reduce | flops 4096 | bytes 32768 | tf_op jit(solution)/shard_map/psum | solution.py:82
  500.2 104.9 %all-gather.11.cloned.1.call-done = bf16[512,8192]{1,0:T(8,128)(2,1)} async-done(((bf16[128,8192]{1,0:T(8,128)(2,1)}), bf16[512,8192]{1,0:T(8,128)(2,1)}) %all-gather.11.cloned.1.call-update) | async-done | bytes 8388624 | tf_op jit(solution)/shard_map/all_gather | solution.py:66
  605.2 131.8 %all-gather.9.cloned.1.call-done = bf16[512,2048]{1,0:T(8,128)(2,1)} async-done(((bf16[128,2048]{1,0:T(8,128)(2,1)}), bf16[512,2048]{1,0:T(8,128)(2,1)}) %all-gather.9.cloned.1.call-update) | async-done | bytes 2097168 | tf_op jit(solution)/shard_map/all_gather | solution.py:65
  737.0 7.2 convolution_bitcast_fusion
  744.2 6.9 copy.40
  751.1 380.2 %all-reduce.9.cloned.1.call-done = f32[4096,1024]{1,0:T(8,128)} async-done(((f32[4096,1024]{1,0:T(8,128)}), f32[4096,1024]{1,0:T(8,128)}) %all-reduce.9.cloned.1.call-update) | async-done | bytes 16777232 | tf_op jit(solution)/shard_map/psum | solution.py:73
  1131.4 12.0 %copy.63 = f32[4096,1024]{1,0:T(8,128)} copy(f32[4096,1024]{1,0:T(8,128)} %all-reduce.9.cloned.1.call-done) | data formatting | bytes 33554432
  (58 shorter events, 49.9 us)
Async XLA Ops:
  8.0 1.6 copy-start.1
  8.0 80.2 %all-gather.7.cloned.1.call-start = ((), (), s32[]{:S(2)}) async-start(), calls=%async_computation.3 | async-start | bytes 6291456 | tf_op jit(solution)/shard_map/all_gather | solution.py:29
  8.7 140.4 %all-gather.5.cloned.1.call-start = ((), (), s32[]{:S(2)}) async-start(), calls=%async_computation.2 | async-start | bytes 10485760 | tf_op jit(solution)/shard_map/all_gather | solution.py:31
  66.7 0.8 copy-start.7
  66.8 170.1 %all-reduce.7.cloned.1.call-start = ((), (), s32[]{:S(2)}) async-start(), calls=%async_computation.4 | async-start | bytes 4194304 | tf_op jit(solution)/shard_map/psum | solution.py:40
  173.7 1.6 copy-start.3
  173.7 86.2 %reduce-scatter.2.cloned.1.call-start = ((), (), s32[]{:S(2)}) async-start(), calls=%async_computation.7 | async-start | bytes 1572864 | tf_op jit(solution)/shard_map/reduce_scatter | solution.py:56
  196.8 102.4 %all-reduce.15.cloned.1.call-start = ((), (), s32[]{:S(2)}) async-start(), calls=%async_computation.11 | async-start | bytes 2097152 | tf_op jit(solution)/shard_map/psum | solution.py:46
  236.9 9.6 copy-start
  250.2 49.0 %copy-start.8 = (f32[1024]{0:T(1024)S(1)}, f32[1024]{0:T(1024)}, u32[]{:S(2)}) copy-start(f32[1024]{0:T(1024)} %param.9) | copy-start | bytes 12292
  260.0 115.4 %all-reduce.11.cloned.1.call-start = ((), (), s32[]{:S(2)}) async-start(), calls=%async_computation.9 | async-start | bytes 4194304 | tf_op jit(solution)/shard_map/psum | solution.py:76
  311.8 145.4 %all-reduce.13.cloned.1.call-start = ((), (), s32[]{:S(2)}) async-start(), calls=%async_computation.10 | async-start | bytes 4194304 | tf_op jit(solution)/shard_map/psum | solution.py:79
  390.1 1.6 copy-start.4
  390.1 215.0 %all-gather.11.cloned.1.call-start = ((), (), s32[]{:S(2)}) async-start(), calls=%async_computation.6 | async-start | bytes 10485760 | tf_op jit(solution)/shard_map/all_gather | solution.py:66
  394.8 1.0 copy-start.6
  394.8 342.1 %all-gather.9.cloned.1.call-start = ((), (), s32[]{:S(2)}) async-start(), calls=%async_computation.5 | async-start | bytes 2621440 | tf_op jit(solution)/shard_map/all_gather | solution.py:65
  403.9 727.5 %all-reduce.9.cloned.1.call-start = ((), (), s32[]{:S(2)}) async-start(), calls=%async_computation.8 | async-start | bytes 33554432 | tf_op jit(solution)/shard_map/psum | solution.py:73
  412.6 1.0 copy-start.5
  440.4 16.8 %copy-start.2 = (bf16[128,64,128]{2,1,0:T(8,128)(2,1)S(1)}, bf16[128,64,128]{2,1,0:T(8,128)(2,1)}, u32[]{:S(2)}) copy-start(bf16[128,64,128]{2,1,0:T(8,128)(2,1)} %param.6) | copy-start | bytes 6291460
Sparse Core Ops, SparseCore 0:
  10.4 77.7 all-gather.6
  90.3 58.7 all-gather.4
  173.9 62.9 all-reduce.6
  239.6 20.3 reduce-scatter.1
  262.8 36.3 all-reduce.14
  311.9 63.4 all-reduce.10
  390.2 50.8 all-reduce.12
  444.3 687.0 all-reduce.8
Sparse Core Ops, SparseCore 1:
  394.9 210.2 all-gather.10
  606.6 130.3 all-gather.8
where the time goes:
time: 1160 us; the launch traced here: 1150 us
  waiting for transfers between devices  846 us (73%)
  blocking collectives  124 us (11%)
  matrix products  109 us (9%)
  local copies, waits for them, and re-layouts  46 us (4%)
  between operations  15.9 us (1%)
    psum x1, waiting for transfers between devices, local(): lax.psum((contract_first(activated, d_pre_b), jnp.sum(d_preact, axis=0)),...  380 us
    all_gather x1, waiting for transfers between devices, local(): lax.all_gather(hidden_all, 'batch', axis=0, tiled=True)  132 us
    all_gather x1, waiting for transfers between devices, local(): lax.all_gather(cot_rows, 'batch', axis=0, tiled=True)  105 us
    psum x1, waiting for transfers between devices, local(): lax.psum(contract_last(d_pre_b, w_in), 'col')  63.5 us
    all_gather x1, waiting for transfers between devices, local(): column_rows = lax.all_gather(regrouped, 'row', axis=2, tiled=True)  60.9 us
    all_to_all x1, blocking collectives, local(): lax.all_to_all(embeddings, 'col', split_axis=2, concat_axis=1, tiled=True)  49.2 us
    psum x1, blocking collectives, local(): lax.psum(jnp.einsum('bde,bdk->ek', emb_float, back_fold, precision=highes...  40.4 us
    psum x1, waiting for transfers between devices, local(): interact = lax.psum(partial_value, 'col')  40.1 us
  transfers between devices with their start and end apart: 10, of which 9 were waited for; matrix products, arithmetic and copies ran while one was open for 9% of the time, Pallas kernels for 0%

commit v1 on v0

--- a/solution.py
+++ b/solution.py
@@ -73,7 +73,9 @@
     grad_in, grad_bias = lax.psum(
         (contract_first(activated, d_pre_b), jnp.sum(d_preact, axis=0)), "batch"
     )
-    d_act = lax.psum(contract_last(d_pre_b, w_in), "col").reshape(tok_rows, emb_local, rank_cols)
+    d_act = jnp.sum(jax.lax.all_gather(contract_last(d_pre_b, w_in), "col"), axis=0).reshape(
+        tok_rows, emb_local, rank_cols
+    )
     inner_term = lax.psum(jnp.sum(d_act * normed, axis=(1, 2)), "row") / feature_count
     d_inter = (inv_rms * (d_act - normed * inner_term[:, None, None])).astype(jnp.bfloat16)
     back_fold = lax.psum(

time: 1160 us -> 1210 us (1.043)
  waiting for transfers between devices: 846 us -> 890 us
    psum x1, waiting for transfers between devices: 380 us -> 523 us  [local(): lax.psum((contract_first(activated, d_pre_b), jnp.sum(d_preact, axis=0)),...]
    all_gather x1, waiting for transfers between devices: 132 us -> 45.5 us  [local(): lax.all_gather(hidden_all, 'batch', axis=0, tiled=True)]
    psum x1 -> x0, waiting for transfers between devices: 63.5 us -> none  [local(): lax.psum(contract_last(d_pre_b, w_in), 'col')]
    all_gather x0 -> x1, waiting for transfers between devices: none -> 41.2 us  [local(): jax.lax.all_gather(contract_last(d_pre_b, w_in), 'col')]
    psum x1, waiting for transfers between devices: 0.01 us -> 38.4 us  [local(): lax.psum(jnp.einsum('bek,bde->bdk', d_inter, embeddings, preferred_elemen...]
    all_gather x1, waiting for transfers between devices: 105 us -> 75.4 us  [local(): lax.all_gather(cot_rows, 'batch', axis=0, tiled=True)]
    unnamed x23 -> x19, local copies, waits for them, and re-layouts: 35.4 us -> 32.8 us
  transfers between devices with their start and end apart: 10 -> 10, of which waited for: 9 -> 10; matrix products, arithmetic and copies ran while one was open for 9% -> 10% of each run, Pallas kernels for 0% -> 0%
where the time goes in v1:
time: 1210 us; the launch traced here: 1200 us
  waiting for transfers between devices  890 us (74%)
  blocking collectives  130 us (11%)
  matrix products  108 us (9%)
  local copies, waits for them, and re-layouts  46.3 us (4%)
  between operations  14.5 us (1%)
  other arithmetic  14 us (1%)
    psum x1, waiting for transfers between devices, local(): lax.psum((contract_first(activated, d_pre_b), jnp.sum(d_preact, axis=0)),...  523 us
    all_gather x1, waiting for transfers between devices, local(): lax.all_gather(cot_rows, 'batch', axis=0, tiled=True)  75.4 us
    all_gather x1, waiting for transfers between devices, local(): column_rows = lax.all_gather(regrouped, 'row', axis=2, tiled=True)  60.9 us
    all_to_all x1, blocking collectives, local(): lax.all_to_all(embeddings, 'col', split_axis=2, concat_axis=1, tiled=True)  49.2 us
    all_gather x1, waiting for transfers between devices, local(): lax.all_gather(hidden_all, 'batch', axis=0, tiled=True)  45.5 us
    all_gather x1, waiting for transfers between devices, local(): jax.lax.all_gather(contract_last(d_pre_b, w_in), 'col')  41.2 us
    psum x1, waiting for transfers between devices, local(): interact = lax.psum(partial_value, 'col')  40.1 us
    psum x1, blocking collectives, local(): lax.psum(jnp.einsum('bde,bdk->ek', emb_float, back_fold, precision=highes...  39.7 us
  transfers between devices with their start and end apart: 10, of which 10 were waited for; matrix products, arithmetic and copies ran while one was open for 10% of the time, Pallas kernels for 0%

profile of v1, /device:TPU:0, one launch (start us, length us, event | category | flops | bytes accessed | tf_op | source)
XLA Modules:
  0.0 1202.7 jit_solution(12258625688629483250)
XLA Ops:
  12.0 49.2 %all_to_all.18 = bf16[128,64,128]{0,1,2:T(8,128)(2,1)S(1)} all-to-all(bf16[128,64,128]{0,1,2:T(8,128)(2,1)} %copy.22), channel_id=1, replica_groups=mesh['batch'=4,'row'=4,'col'=2] {'col'}, dimensions={2} | all-to-all | bytes 4194304 | tf_op jit(solution)/shard_map/all_to_all | solution.py:30
  66.9 20.5 %all-gather.9.cloned.1.call-done = bf16[128,128,128]{2,1,0:T(8,128)(2,1)} async-done(((bf16[128,64,128]{2,1,0:T(8,128)(2,1)}), bf16[128,128,128]{2,1,0:T(8,128)(2,1)}) %all-gather.9.cloned.1.call-update) | async-done | bytes 4194320 | tf_op jit(solution)/shard_map/all_gather | solution.py:29
  87.3 60.9 %all-gather.7.cloned.1.call-done = bf16[128,128,256]{1,2,0:T(8,128)(2,1)} async-done(((bf16[128,128,64]{1,2,0:T(8,128)(2,1)}), bf16[128,128,256]{1,2,0:T(8,128)(2,1)}) %all-gather.7.cloned.1.call-update) | async-done | bytes 8388624 | tf_op jit(solution)/shard_map/all_gather | solution.py:31
  148.3 13.1 %fusion.24 = f32[128,256,128]{2,1,0:T(8,128)} fusion(bf16[128,128,256]{1,2,0:T(8,128)(2,1)} %all-gather.7.cloned.1.call-done, bf16[128,128,128]{2,1,0:T(8,128)(2,1)} %all-gather.9.cloned.1.call-done), kind=kOutput, calls=%fused_computation.32 | convolution fusion | flops 1073741824 | bytes 29360128 | tf_op jit(solution)/shard_map/bdj,bde->bje/dot_general | solution.py:32
  161.3 11.5 fusion.25
  174.5 21.4 %fusion.8 = f32[128,2048]{1,0:T(8,128)} fusion(bf16[2048,64,128]{2,1,0:T(8,128)(2,1)} %param.10, bf16[128,64,128]{2,1,0:T(8,128)(2,1)S(1)} %copy-done.3), kind=kOutput, calls=%fused_computation.7 | convolution fusion | flops 4294967296 | bytes 36700160 | tf_op jit(solution)/shard_map/dot_general | solution.py:16
  196.0 40.1 %all-reduce.6.cloned.1.call-done = f32[128,128,32]{1,2,0:T(8,128)} async-done(((f32[128,128,32]{1,2,0:T(8,128)}), f32[128,128,32]{1,2,0:T(8,128)}) %all-reduce.6.cloned.1.call-update) | async-done | bytes 2097168 | tf_op jit(solution)/shard_map/psum | solution.py:40
  238.8 6.8 psum.64
  259.2 39.2 %all-reduce.12.cloned.1.call-done = (f32[128,1024]{1,0:T(8,128)}, f32[128,1024]{1,0:T(8,128)}) async-done(((f32[128,1024]{1,0:T(8,128)}, f32[128,1024]{1,0:T(8,128)}), (f32[128,1024]{1,0:T(8,128)}, f32[128,1024]{1,0:T(8,128)})) %all-reduce.12.cloned.1.call-update) | async-done | bytes 1048592 | tf_op jit(solution)/shard_map/psum | solution.py:46
  300.5 7.6 fusion.18
  312.9 13.6 %all_gather.23 = bf16[128,2048]{1,0:T(8,128)(2,1)} all-gather(bf16[128,1024]{1,0:T(8,128)(2,1)} %get-tuple-element.9), channel_id=1, replica_groups=mesh['batch'=4,'row'=4,'col'=2] {'col'}, dimensions={1}, use_global_device_ids=true | all-gather | bytes 786432 | tf_op jit(solution)/shard_map/all_gather | solution.py:48
  326.6 41.2 %all-gather.15.cloned.1.call-done = f32[256,4096]{1,0:T(8,128)} async-done(((f32[128,4096]{1,0:T(8,128)}), f32[256,4096]{1,0:T(8,128)}) %all-gather.15.cloned.1.call-update) | async-done | bytes 4194320 | tf_op jit(solution)/shard_map/all_gather | solution.py:76
  381.9 7.0 psum.69
  394.0 8.5 fusion.20
  403.5 25.7 %fusion.12 = bf16[16,8,64,128]{3,1,2,0:T(8,128)(2,1)S(1)} fusion(bf16[128,2048]{1,0:T(8,128)(2,1)S(1)} %copy-done.4, bf16[256,8,64,128]{3,2,1,0:T(8,128)(2,1)} %bitcast.62), kind=kOutput, calls=%fused_computation.14 | convolution fusion | flops 4296015872 | bytes 36175872 | tf_op jit(solution)/shard_map/dot_general | solution.py:51
  431.2 13.2 %psum.68 = f32[1024]{0:T(1024)} all-reduce(f32[1024]{0:T(1024)S(1)} %get-tuple-element.7), channel_id=1, replica_groups=mesh['batch'=4,'row'=4,'col'=2] {'batch'}, use_global_device_ids=true, to_apply=%region_8.9 | all-reduce | flops 1024 | bytes 8192 | tf_op jit(solution)/shard_map/psum | solution.py:73
  444.4 75.4 %all-gather.13.cloned.1.call-done = bf16[512,8192]{1,0:T(8,128)(2,1)} async-done(((bf16[128,8192]{1,0:T(8,128)(2,1)}), bf16[512,8192]{1,0:T(8,128)(2,1)}) %all-gather.13.cloned.1.call-update) | async-done | bytes 8388624 | tf_op jit(solution)/shard_map/all_gather | solution.py:66
  519.8 45.5 %all-gather.11.cloned.1.call-done = bf16[512,2048]{1,0:T(8,128)(2,1)} async-done(((bf16[128,2048]{1,0:T(8,128)(2,1)}), bf16[512,2048]{1,0:T(8,128)(2,1)}) %all-gather.11.cloned.1.call-update) | async-done | bytes 2097168 | tf_op jit(solution)/shard_map/all_gather | solution.py:65
  565.3 7.2 convolution_bitcast_fusion
  572.6 6.9 copy.40
  579.5 38.4 %all-reduce.10.cloned.1.call-done = f32[128,64,32]{1,2,0:T(8,128)} async-done(((f32[128,64,32]{1,2,0:T(8,128)}), f32[128,64,32]{1,2,0:T(8,128)}) %all-reduce.10.cloned.1.call-update) | async-done | bytes 1048592 | tf_op jit(solution)/shard_map/psum | solution.py:81
  620.6 39.7 %psum.71 = f32[128,32]{0,1:T(8,128)} all-reduce(f32[128,32]{0,1:T(8,128)S(1)} %convolution_bitcast_fusion.2), channel_id=1, replica_groups=mesh['batch'=4,'row'=4,'col'=2] {'batch','col'}, use_global_device_ids=true, to_apply=%region_13.14 | all-reduce | flops 4096 | bytes 32768 | tf_op jit(solution)/shard_map/psum | solution.py:84
  660.3 523.4 %all-reduce.8.cloned.1.call-done = f32[4096,1024]{1,0:T(8,128)} async-done(((f32[4096,1024]{1,0:T(8,128)}), f32[4096,1024]{1,0:T(8,128)}) %all-reduce.8.cloned.1.call-update) | async-done | bytes 16777232 | tf_op jit(solution)/shard_map/psum | solution.py:73
  1183.7 12.0 copy.62
  (56 shorter events, 60.1 us)
Async XLA Ops:
  7.2 1.6 copy-start.1
  7.2 80.2 %all-gather.9.cloned.1.call-start = ((), (), s32[]{:S(2)}) async-start(), calls=%async_computation.3 | async-start | bytes 6291456 | tf_op jit(solution)/shard_map/all_gather | solution.py:29
  7.9 140.4 %all-gather.7.cloned.1.call-start = ((), (), s32[]{:S(2)}) async-start(), calls=%async_computation.2 | async-start | bytes 10485760 | tf_op jit(solution)/shard_map/all_gather | solution.py:31
  65.9 0.8 copy-start.5
  65.9 170.1 %all-reduce.6.cloned.1.call-start = ((), (), s32[]{:S(2)}) async-start(), calls=%async_computation.4 | async-start | bytes 4194304 | tf_op jit(solution)/shard_map/psum | solution.py:40
  172.9 1.6 copy-start.3
  172.9 86.2 %reduce-scatter.2.cloned.1.call-start = ((), (), s32[]{:S(2)}) async-start(), calls=%async_computation.7 | async-start | bytes 1572864 | tf_op jit(solution)/shard_map/reduce_scatter | solution.py:56
  195.9 102.4 %all-reduce.12.cloned.1.call-start = ((), (), s32[]{:S(2)}) async-start(), calls=%async_computation.11 | async-start | bytes 2097152 | tf_op jit(solution)/shard_map/psum | solution.py:46
  236.1 9.6 copy-start
  249.4 49.0 %copy-start.6 = (f32[1024]{0:T(1024)S(1)}, f32[1024]{0:T(1024)}, u32[]{:S(2)}) copy-start(f32[1024]{0:T(1024)} %param.9) | copy-start | bytes 12292
  259.2 108.7 %all-gather.15.cloned.1.call-start = ((), (), s32[]{:S(2)}) async-start(), calls=%async_computation.10 | async-start | bytes 6291456 | tf_op jit(solution)/shard_map/all_gather | solution.py:76
  308.1 211.7 %all-gather.13.cloned.1.call-start = ((), (), s32[]{:S(2)}) async-start(), calls=%async_computation.6 | async-start | bytes 10485760 | tf_op jit(solution)/shard_map/all_gather | solution.py:66
  312.9 252.4 %all-gather.11.cloned.1.call-start = ((), (), s32[]{:S(2)}) async-start(), calls=%async_computation.5 | async-start | bytes 2621440 | tf_op jit(solution)/shard_map/all_gather | solution.py:65
  326.6 291.3 %all-reduce.10.cloned.1.call-start = ((), (), s32[]{:S(2)}) async-start(), calls=%async_computation.9 | async-start | bytes 4194304 | tf_op jit(solution)/shard_map/psum | solution.py:81
  393.8 789.9 %all-reduce.8.cloned.1.call-start = ((), (), s32[]{:S(2)}) async-start(), calls=%async_computation.8 | async-start | bytes 33554432 | tf_op jit(solution)/shard_map/psum | solution.py:73
  402.5 1.0 copy-start.4
  572.5 45.3 %copy-start.2 = (bf16[128,64,128]{2,1,0:T(8,128)(2,1)S(1)}, bf16[128,64,128]{2,1,0:T(8,128)(2,1)}, u32[]{:S(2)}) copy-start(bf16[128,64,128]{2,1,0:T(8,128)(2,1)} %param.6) | copy-start | bytes 6291460
Sparse Core Ops, SparseCore 0:
  9.5 77.7 all-gather.8
  89.5 58.7 all-gather.6
  173.0 62.9 all-reduce.5
  238.7 20.3 reduce-scatter.1
  262.0 36.3 all-reduce.11
  308.2 59.5 all-gather.14
  370.0 149.7 all-gather.12
  521.4 43.8 all-gather.10
  567.7 50.1 all-reduce.9
  620.8 562.8 all-reduce.7
